TPU v7x, 32 devices: a whole 2x2x4 slice. The times are simulated.
32 devices in a mesh: seq: 4 (over y, x), mem: 8 (over z, core).
Axes of the slice: x: 2, y: 2, z: 4, core: 2. Of those that a mesh axis runs over, the one named last changes fastest.
Arguments:
- hidden: bfloat16 [8192, 2048], P(('seq', 'mem')), may hold values from -6 to 6
- routes: int32 [8192, 2], P(('seq', 'mem')), may hold values from 0 to 7, all different within a row; in each aligned block of 256 rows (0 to 255, 256 to 511, ...) at most 64 rows name the same one
- gate_levels: int32 [8192, 2], P(('seq', 'mem')), may hold values from 1 to 255
- query_weight: bfloat16 [2048, 1024], P('seq'), may hold values from -0.125 to 0.125
- key_weight: bfloat16 [8, 2048, 1024], P('mem', 'seq'), may hold values from -0.125 to 0.125
- value_weight: bfloat16 [8, 2048, 1024], P('mem', 'seq'), may hold values from -0.125 to 0.125
Outputs:
- mixed: bfloat16 [8192, 1024], P(('seq', 'mem'))
Inputs may be any that keep to these rules, and one draw needn't show every extreme that they name: `routes`: the two memories of a row differ. In the rows of one device no memory is named by more than 64 rows, a bound that some block reaches.
All inputs are finite; a program needn't handle non-finite values.
Results may differ from a plain program's by a relative error of at most 0.01.
Values may be sent and summed in bfloat16 or wider, within the bound.
No kernel may reach another device: no remote copies, remote signals or barrier semaphores. Data moves between devices by JAX's collectives and lax.ppermute only.
A program may use at most 128 MiB of HBM per device.

v0:
```python
import jax
import jax.numpy as jnp
from jax import lax
from jax.sharding import PartitionSpec as P

HEADS = 8
DK = 128
BLOCK = 512
CAP = 64


def entering(array, axis, join, neutral):
    place = lax.axis_index(axis)
    gathered = lax.all_gather(array.astype(jnp.bfloat16), axis)
    state = jnp.zeros_like(array) + jnp.asarray(neutral, array.dtype)

    def one(step, state):
        return join(state, lax.dynamic_index_in_dim(gathered, step, 0, False).astype(array.dtype))

    return lax.fori_loop(0, place, one, state)


def add_states(earlier, later):
    return earlier + later


def on_device(hidden, routes, gate_levels, query_weight, key_weight, value_weight):
    count = hidden.shape[0]
    model = hidden.shape[1]
    width = query_weight.shape[1]
    mem_local = key_weight.shape[0]
    experts = mem_local * lax.axis_size("mem")
    highest = lax.Precision.HIGHEST
    onehot = (routes[:, :, None] == jnp.arange(experts, dtype=jnp.int32)[None, None, :]).astype(
        jnp.int32
    )
    per_token = jnp.sum(onehot, axis=1)
    before = jnp.cumsum(per_token, axis=0) - per_token
    place = jnp.sum(onehot * before[:, None, :], axis=2)
    slots = (routes * CAP + place).reshape(-1)
    owner_of = jnp.arange(2 * count, dtype=jnp.int32) // 2
    match = jnp.arange(experts * CAP, dtype=jnp.int32)[:, None] == slots[None, :]
    source = jnp.sum(jnp.where(match, owner_of[None, :], 0), axis=1)
    filled = jnp.any(match, axis=1)
    sent_rows = jnp.where(
        filled[:, None], jnp.take(hidden, source, axis=0), jnp.zeros((), hidden.dtype)
    )
    sent_rows = sent_rows.reshape(experts, CAP, model)
    columns = hidden
    queries = jnp.dot(
        columns,
        lax.all_gather(query_weight, "seq", axis=0, tiled=True),
        preferred_element_type=jnp.float32,
    ).astype(jnp.bfloat16)
    sent_queries = jnp.where(
        filled[:, None], jnp.take(queries, source, axis=0), jnp.zeros((), queries.dtype)
    )
    sent_queries = sent_queries.reshape(experts, CAP, width)
    arrived, arrived_queries = (
        lax.all_to_all(sent_rows, "mem", split_axis=0, concat_axis=1, tiled=True),
        lax.all_to_all(sent_queries, "mem", split_axis=0, concat_axis=1, tiled=True),
    )
    length = arrived.shape[1]
    columns = arrived
    key_part = jnp.einsum(
        "mrc,mch->mrh",
        columns,
        lax.all_gather(key_weight, "seq", axis=1, tiled=True),
        preferred_element_type=jnp.float32,
    )
    value_part = jnp.einsum(
        "mrc,mch->mrh",
        columns,
        lax.all_gather(value_weight, "seq", axis=1, tiled=True),
        preferred_element_type=jnp.float32,
    )
    keys = key_part
    values = value_part
    keys = keys.astype(jnp.bfloat16)
    values = values.astype(jnp.bfloat16)
    nblocks = length // BLOCK
    shape5 = (mem_local, nblocks, BLOCK, HEADS, DK)
    q_five = arrived_queries.reshape(shape5)
    k_five = keys.reshape(shape5)
    v_five = values.reshape(shape5)
    block_states = jnp.einsum(
        "mnkhd,mnkhe->mnhde", k_five, v_five, preferred_element_type=jnp.float32
    )
    within = jnp.cumsum(block_states, axis=1) - block_states
    local_total = jnp.sum(block_states, axis=1)
    nothing = jnp.zeros_like(local_total)
    incoming = entering(local_total, "seq", add_states, nothing)
    states = (incoming[:, None] + within).reshape(mem_local * nblocks, HEADS, DK, DK)
    flat = (mem_local * nblocks, BLOCK, HEADS, DK)
    rowids = jnp.arange(BLOCK, dtype=jnp.int32)
    causal = (rowids[:, None] >= rowids[None, :]).astype(jnp.float32)

    def attend(inputs):
        q_block, k_block, v_block, state = inputs
        scores = (
            jnp.einsum("qhd,khd->hqk", q_block, k_block, preferred_element_type=jnp.float32)
            * causal[None]
        )
        local = jnp.einsum("hqk,khd->qhd", scores, v_block.astype(jnp.float32), precision=highest)
        carried = jnp.einsum("qhd,hde->qhe", q_block.astype(jnp.float32), state, precision=highest)
        reads = local + carried
        scale = lax.rsqrt(jnp.mean(reads * reads, axis=-1, keepdims=True) + 1e-06)
        return (reads * scale).astype(jnp.bfloat16)

    normed = lax.map(
        attend, (q_five.reshape(flat), k_five.reshape(flat), v_five.reshape(flat), states)
    )
    normed = normed.reshape(mem_local, length, width)
    returned = lax.all_to_all(normed, "mem", split_axis=1, concat_axis=0, tiled=True)
    returned = returned.reshape(experts * CAP, width)
    picked = jnp.take(returned, slots, axis=0).reshape(count, 2, width)
    levels = gate_levels.astype(jnp.float32)
    gates = levels / jnp.sum(levels, axis=1, keepdims=True)
    mixed = jnp.sum(gates[:, :, None] * picked.astype(jnp.float32), axis=1)
    return mixed.astype(jnp.bfloat16)


def solution(mesh):
    return jax.shard_map(
        on_device,
        mesh=mesh,
        in_specs=(
            P(("seq", "mem"), None),
            P(("seq", "mem"), None),
            P(("seq", "mem"), None),
            P("seq", None),
            P("mem", "seq", None),
            P("mem", "seq", None),
        ),
        out_specs=P(("seq", "mem"), None),
        check_vma=False,
    )
```

profile of v0, /device:TPU:0, one launch (start us, length us, event | category | flops | bytes accessed | tf_op | source)
XLA Modules:
  0.0 289.7 jit_solution(13704537950358973058)
XLA Ops:
  6.5 0.0 copy-start
  6.5 0.0 all-gather.10.cloned.1.call-start
  6.5 0.7 all-gather.10.cloned.1.call-update
  7.3 0.0 all-gather.6.cloned.1.call-start
  7.3 0.7 all-gather.6.cloned.1.call-update
  8.0 0.0 all-gather.8.cloned.1.call-start
  8.1 0.7 all-gather.8.cloned.1.call-update
  8.7 0.0 all-gather.12.cloned.1.call-start
  8.8 0.0 copy-done.5
  8.8 0.6 reduce-window.6
  9.4 0.2 slice_reduce_fusion
  9.7 0.1 bitcast_subtract_fusion
  9.8 0.1 copy.61
  9.9 0.1 reshape.211
  10.1 0.2 fusion.24
  10.3 0.2 select_reduce_fusion
  10.5 0.1 reduce_sum.67
  10.5 0.1 broadcast_in_dim.94
  10.6 0.0 copy-done
  10.6 2.5 gather_fusion
  13.1 0.3 select_select_fusion
  13.5 55.2 %all_to_all.12 = bf16[8,64,2048]{2,1,0:T(8,128)(2,1)S(1)} all-to-all(bf16[8,64,2048]{2,1,0:T(8,128)(2,1)S(1)} %select_select_fusion), channel_id=1, replica_groups=mesh['seq'=4,'mem'=8] {'mem'}, dimensions={0} | all-to-all | bytes 4194304 | tf_op jit(solution)/shard_map/all_to_all | solution.py:60
  68.7 1.4 copy-done.4
  70.0 5.5 %fusion.15 = bf16[512,1024]{1,0:T(8,128)(2,1)} fusion(bf16[512,2048]{1,0:T(8,128)(2,1)S(1)} %bitcast.80, bf16[1,2048,1024]{2,1,0:T(8,128)(2,1)} %all-gather.10.cloned.1.call-done), kind=kOutput, calls=%fused_computation.20 | convolution fusion | flops 2148007936 | bytes 7340032 | tf_op jit(solution)/shard_map/mrc,mch->mrh/dot_general | solution.py:65
  75.5 1.6 copy.74
  77.1 41.9 %all-gather.6.cloned.1.call-done = bf16[1,2048,1024]{2,1,0:T(8,128)(2,1)} async-done(((bf16[1,512,1024]{2,1,0:T(8,128)(2,1)}), bf16[1,2048,1024]{2,1,0:T(8,128)(2,1)}) %all-gather.6.cloned.1.call-update) | async-done | bytes 4194320 | tf_op jit(solution)/shard_map/all_gather | solution.py:74
  119.0 5.2 %fusion.18 = bf16[64,8,8,128]{3,2,1,0:T(8,128)(2,1)S(1)} fusion(bf16[512,2048]{1,0:T(8,128)(2,1)} %bitcast.81, bf16[1,2048,1024]{2,1,0:T(8,128)(2,1)} %all-gather.6.cloned.1.call-done), kind=kOutput, calls=%fused_computation.21 | convolution fusion | flops 2148007936 | bytes 7340032 | tf_op jit(solution)/shard_map/mrc,mch->mrh/dot_general | solution.py:71
  124.2 0.0 copy-start.2
  124.2 1.0 copy-done.2
  125.2 1.2 fusion.36
  126.3 0.0 all-gather.12.cloned.1.call-update
  126.3 47.1 %all-gather.8.cloned.1.call-done = bf16[2048,1024]{1,0:T(8,128)(2,1)} async-done(((bf16[512,1024]{1,0:T(8,128)(2,1)}), bf16[2048,1024]{1,0:T(8,128)(2,1)}) %all-gather.8.cloned.1.call-update) | async-done | bytes 4194320 | tf_op jit(solution)/shard_map/all_gather | solution.py:52
  173.5 3.4 %convolution_convert_fusion = bf16[256,1024]{1,0:T(8,128)(2,1)S(1)} fusion(bf16[256,2048]{1,0:T(8,128)(2,1)S(1)} %copy-done, bf16[2048,1024]{1,0:T(8,128)(2,1)} %all-gather.8.cloned.1.call-done), kind=kOutput, calls=%fused_computation.22 | convolution fusion | flops 1074003968 | bytes 5767168 | tf_op jit(solution)/shard_map/dot_general | solution.py:50
  176.9 2.8 gather_fusion.1
  179.7 2.4 select_select_fusion.1
  182.1 4.6 %all-to-all-start.1 = ((bf16[8,64,1024]{2,1,0:T(8,128)(2,1)}), bf16[8,64,1024]{2,1,0:T(8,128)(2,1)}, u32[]{:S(2)}, u32[]{:S(2)}) async-start(bf16[8,64,1024]{2,1,0:T(8,128)(2,1)} %select_select_fusion.1), calls=%async_computation.1 | async-start | bytes 2097152 | tf_op jit(solution)/shard_map/all_to_all | solution.py:61
  186.7 1.1 fusion.25
  187.8 13.9 %all-gather.12.cloned.1.call-done = bf16[32,128,128]{2,1,0:T(8,128)(2,1)} async-done(((bf16[8,128,128]{2,1,0:T(8,128)(2,1)}), bf16[32,128,128]{2,1,0:T(8,128)(2,1)}) %all-gather.12.cloned.1.call-update) | async-done | bytes 1048592 | tf_op jit(solution)/shard_map/all_gather | solution.py:14
  201.7 0.2 while.2
  201.9 11.5 %all-to-all-done.1 = bf16[8,64,1024]{2,1,0:T(8,128)(2,1)} async-done(((bf16[8,64,1024]{2,1,0:T(8,128)(2,1)}), bf16[8,64,1024]{2,1,0:T(8,128)(2,1)}, u32[]{:S(2)}, u32[]{:S(2)}) %all-to-all-start.1) | async-done | bytes 1048608 | tf_op jit(solution)/shard_map/all_to_all | solution.py:61
  213.4 1.5 copy.76
  214.9 1.2 fusion.30
  216.1 0.0 copy-start.1
  216.2 0.0 copy-start.3
  216.2 1.1 fusion.28
  217.2 0.1 copy-done.1
  217.4 0.3 copy-done.3
  217.7 5.5 %fusion.7 = (f32[512,8]{0,1:T(8,128)S(1)}, f32[8,128,512]{2,1,0:T(8,128)S(1)}) fusion(f32[8,128,512]{2,1,0:T(8,128)S(1)} %fusion.28, f32[8,512,512]{2,1,0:T(8,128)S(1)} %fusion.30, f32[512,512]{1,0:T(8,128)S(1)} %copy-done.1, bf16[64,8,8,128]{3,2,1,0:T(8,128)(2,1)S(1)} %copy-done.3), kind=kOutput, calls=%fused_computation.13 | convolution fusion | flops 3224891392 | bytes 14696448 | tf_op jit(solution)/shard_map/while/body/eval_jaxpr/hqk,khd->qhd/dot_general | solution.py:104
  223.2 1.3 fusion.8
  224.5 4.7 %copy.70 = bf16[1,512,1024]{2,0,1:T(2,128)(2,1)S(1)} copy(bf16[1,512,1024]{1,2,0:T(8,128)(2,1)} %bitcast.78) | data formatting | bytes 2097152 | tf_op jit(solution)/shard_map/reshape | solution.py:113
  229.2 0.5 broadcast.156
  229.8 7.8 %reduce.2 = bf16[512,1024]{1,0:T(8,128)(2,1)} reduce(bf16[512,1,1024]{2,1,0:T(2,128)(2,1)S(1)} %bitcast.77, bf16[]{:T(256)} %broadcast.156), dimensions={1}, to_apply=%bitcast.55.reduce_sub_computation | reduce | bytes 2097154
  237.5 2.6 reshape.245
  240.2 3.6 %all-to-all-start.2 = ((bf16[8,2,32768]{2,1,0:T(2,128)(2,1)}), bf16[8,2,32768]{2,1,0:T(2,128)(2,1)S(1)}, u32[]{:S(2)}, u32[]{:S(2)}) async-start(bf16[8,2,32768]{2,1,0:T(2,128)(2,1)} %reshape.245), calls=%async_computation.2 | async-start | bytes 2097152 | tf_op jit(solution)/shard_map/all_to_all | solution.py:114
  243.7 0.1 reshape.217
  243.9 0.2 copy.60
  244.1 0.0 copy-done.6
  244.1 0.1 copy.59
  244.3 26.0 %all-to-all-done.2 = bf16[8,2,32768]{2,1,0:T(2,128)(2,1)S(1)} async-done(((bf16[8,2,32768]{2,1,0:T(2,128)(2,1)}), bf16[8,2,32768]{2,1,0:T(2,128)(2,1)S(1)}, u32[]{:S(2)}, u32[]{:S(2)}) %all-to-all-start.2) | async-done | bytes 1048608 | tf_op jit(solution)/shard_map/all_to_all | solution.py:114
  270.2 3.5 %reshape.246 = bf16[512,1,1024]{2,1,0:T(2,128)(2,1)} reshape(bf16[8,2,32768]{2,1,0:T(2,128)(2,1)S(1)} %all-to-all-done.2) | data formatting | bytes 2097152
  273.7 2.0 copy.94
  275.6 2.1 gather_fusion.2
  277.7 0.4 gather.23
  278.2 5.0 %multiply_reduce_fusion = bf16[256,1024]{1,0:T(8,128)(2,1)} fusion(bf16[256,2,1024]{2,1,0:T(2,128)(2,1)S(1)} %gather.23, pred[256,2]{1,0:T(8,128)(4,1)S(1)} %copy.60, f32[256,2]{1,0:T(8,128)S(1)} %copy.59), kind=kLoop, calls=%fused_computation.15 | loop fusion | flops 1835008 | bytes 1575424 | tf_op jit(solution)/shard_map/reduce_sum | solution.py:119
  (19 shorter events, 0.2 us)
Async XLA Ops:
  6.5 4.1 %copy-start = (bf16[256,2048]{1,0:T(8,128)(2,1)S(1)}, bf16[256,2048]{1,0:T(8,128)(2,1)}, u32[]{:S(2)}) copy-start(bf16[256,2048]{1,0:T(8,128)(2,1)} %param.8) | copy-start | bytes 3145732
  6.5 2.3 copy-start.5
  6.5 62.1 %all-gather.10.cloned.1.call-start = ((), (), s32[]{:S(2)}) async-start(), calls=%async_computation.5 | async-start | bytes 5242880 | tf_op jit(solution)/shard_map/all_gather | solution.py:68
  7.3 111.8 %all-gather.6.cloned.1.call-start = ((), (), s32[]{:S(2)}) async-start(), calls=%async_computation.3 | async-start | bytes 5242880 | tf_op jit(solution)/shard_map/all_gather | solution.py:74
  8.0 165.5 %all-gather.8.cloned.1.call-start = ((), (), s32[]{:S(2)}) async-start(), calls=%async_computation.4 | async-start | bytes 5242880 | tf_op jit(solution)/shard_map/all_gather | solution.py:52
  8.7 193.0 %all-gather.12.cloned.1.call-start = ((), (), s32[]{:S(2)}) async-start(), calls=%async_computation.6 | async-start | bytes 1310720 | tf_op jit(solution)/shard_map/all_gather | solution.py:14
  68.7 1.4 copy-start.4
  124.2 1.0 copy-start.2
  182.1 31.3 %all-to-all-start.1 = ((bf16[8,64,1024]{2,1,0:T(8,128)(2,1)}), bf16[8,64,1024]{2,1,0:T(8,128)(2,1)}, u32[]{:S(2)}, u32[]{:S(2)}) async-start(bf16[8,64,1024]{2,1,0:T(8,128)(2,1)} %select_select_fusion.1), calls=%async_computation.1 | async-start | bytes 2097152 | tf_op jit(solution)/shard_map/all_to_all | solution.py:61
  216.1 1.2 copy-start.1
  216.2 1.5 copy-start.3
  237.5 6.5 %copy-start.6 = (s32[256,2]{0,1:T(2,128)S(1)}, s32[256,2]{0,1:T(2,128)}, u32[]{:S(2)}) copy-start(s32[256,2]{0,1:T(2,128)} %param.10) | copy-start | bytes 6148
  240.2 30.1 %all-to-all-start.2 = ((bf16[8,2,32768]{2,1,0:T(2,128)(2,1)}), bf16[8,2,32768]{2,1,0:T(2,128)(2,1)S(1)}, u32[]{:S(2)}, u32[]{:S(2)}) async-start(bf16[8,2,32768]{2,1,0:T(2,128)(2,1)} %reshape.245), calls=%async_computation.2 | async-start | bytes 2097152 | tf_op jit(solution)/shard_map/all_to_all | solution.py:114
Sparse Core Ops, SparseCore 0:
  9.2 55.3 all-gather.9
  66.4 52.5 all-gather.5
  120.9 52.5 all-gather.7
  175.2 26.4 all-gather.11
where the time goes:
time: 290 us
  waiting for transfers between devices  142 us (49%)
  blocking collectives  55.2 us (19%)
  local copies, waits for them, and re-layouts  28.1 us (10%)
  matrix products  23 us (8%)
  other arithmetic  19.1 us (7%)
  between operations  13.4 us (5%)
  starting transfers between devices  8.28 us (3%)
    all_to_all x1, blocking collectives, on_device(): lax.all_to_all(sent_rows, 'mem', split_axis=0, concat_axis=1, tiled=True)  55.2 us
    all_gather x1, waiting for transfers between devices, on_device(): lax.all_gather(query_weight, 'seq', axis=0, tiled=True)  47.1 us
    all_gather x1, waiting for transfers between devices, on_device(): lax.all_gather(value_weight, 'seq', axis=1, tiled=True)  41.9 us
    all_to_all x1, waiting for transfers between devices, on_device(): lax.all_to_all(normed, 'mem', split_axis=1, concat_axis=0, tiled=True)  26 us
    all_gather x1, waiting for transfers between devices, entering(): gathered = lax.all_gather(array.astype(jnp.bfloat16), axis)  13.9 us
    unnamed x19, local copies, waits for them, and re-layouts  12.9 us
    all_to_all x1, waiting for transfers between devices, on_device(): lax.all_to_all(sent_queries, 'mem', split_axis=0, concat_axis=1, tiled=True)  11.5 us
    unnamed x1, other arithmetic  7.77 us
  transfers between devices with their start and end apart: 6, of which 5 were waited for; matrix products, arithmetic and copies ran while one was open for 10% of the time, Pallas kernels for 0%

commit v1 on v0

--- a/solution.py
+++ b/solution.py
@@ -2,6 +2,7 @@
 import jax.numpy as jnp
 from jax import lax
 from jax.sharding import PartitionSpec as P
+from jax.lax import axis_index, axis_size, ppermute
 
 HEADS = 8
 DK = 128
@@ -68,12 +69,23 @@
         lax.all_gather(key_weight, "seq", axis=1, tiled=True),
         preferred_element_type=jnp.float32,
     )
-    value_part = jnp.einsum(
-        "mrc,mch->mrh",
-        columns,
-        lax.all_gather(value_weight, "seq", axis=1, tiled=True),
-        preferred_element_type=jnp.float32,
-    )
+    answer = axis_size("seq")
+    known = axis_index("seq")
+    taken_in, block_out, back = (answer, known, value_weight.shape[1])
+    items = tuple(((tick, (tick + 1) % taken_in) for tick in range(taken_in)))
+    res, value_part = (value_weight, None)
+    for c in range(taken_in):
+        local_part = ppermute(res, "seq", items) if c < taken_in - 1 else None
+        found_now = jnp.einsum(
+            "mrc,mch->mrh",
+            lax.dynamic_slice_in_dim(
+                columns, (block_out - c) % taken_in * back, res.shape[1], axis=2
+            ),
+            res,
+            preferred_element_type=jnp.float32,
+        )
+        value_part = found_now if value_part is None else value_part + found_now
+        res = local_part
     keys = key_part
     values = value_part
     keys = keys.astype(jnp.bfloat16)

time: 290 us -> 279 us (0.962)
  blocking collectives: 55.2 us -> 0 us
  waiting for transfers between devices: 142 us -> 175 us
  starting transfers between devices: 8.28 us -> 16 us
  matrix products: 23 us -> 26.5 us
    ppermute x0 -> x3, waiting for transfers between devices: none -> 114 us  [on_device(): local_part = ppermute(res, 'seq', items) if c < taken_in - 1 else None]
    all_to_all x1 -> x0, blocking collectives: 55.2 us -> none  [on_device(): lax.all_to_all(sent_rows, 'mem', split_axis=0, concat_axis=1, tiled=True)]
    all_gather x1 -> x0, waiting for transfers between devices: 41.9 us -> none  [on_device(): lax.all_gather(value_weight, 'seq', axis=1, tiled=True)]
    all_gather x1, waiting for transfers between devices: 47.1 us -> 7.64 us  [on_device(): lax.all_gather(query_weight, 'seq', axis=0, tiled=True)]
    all_to_all x0 -> x1, starting transfers between devices: none -> 6.35 us  [on_device(): lax.all_to_all(sent_rows, 'mem', split_axis=0, concat_axis=1, tiled=True)]
    dot_general x1 -> x4, matrix products: 5.15 us -> 7.7 us  [on_device(): jnp.einsum('mrc,mch->mrh', lax.dynamic_slice_in_dim(columns, (block_out -...]
    unnamed x19 -> x25, local copies, waits for them, and re-layouts: 12.9 us -> 11.3 us
  transfers between devices with their start and end apart: 6 -> 9, of which waited for: 5 -> 7; matrix products, arithmetic and copies ran while one was open for 10% -> 12% of each run, Pallas kernels for 0% -> 0%
where the time goes in v1:
time: 279 us; the launch traced here: 278 us
  waiting for transfers between devices  175 us (63%)
  matrix products  26.5 us (9%)
  local copies, waits for them, and re-layouts  26.4 us (9%)
  other arithmetic  20.5 us (7%)
  starting transfers between devices  16 us (6%)
  between operations  13.4 us (5%)
    ppermute x3, waiting for transfers between devices, on_device(): local_part = ppermute(res, 'seq', items) if c < taken_in - 1 else None  114 us
    all_to_all x1, waiting for transfers between devices, on_device(): lax.all_to_all(normed, 'mem', split_axis=1, concat_axis=0, tiled=True)  26 us
    all_gather x1, waiting for transfers between devices, entering(): gathered = lax.all_gather(array.astype(jnp.bfloat16), axis)  13.1 us
    all_to_all x1, waiting for transfers between devices, on_device(): lax.all_to_all(sent_queries, 'mem', split_axis=0, concat_axis=1, tiled=True)  12.2 us
    unnamed x25, local copies, waits for them, and re-layouts  11.3 us
    unnamed x1, other arithmetic  7.77 us
    dot_general x4, matrix products, on_device(): jnp.einsum('mrc,mch->mrh', lax.dynamic_slice_in_dim(columns, (block_out -...  7.7 us
    all_gather x1, waiting for transfers between devices, on_device(): lax.all_gather(query_weight, 'seq', axis=0, tiled=True)  7.64 us
  transfers between devices with their start and end apart: 9, of which 7 were waited for; matrix products, arithmetic and copies ran while one was open for 12% of the time, Pallas kernels for 0%

profile of v1, /device:TPU:0, one launch (start us, length us, event | category | flops | bytes accessed | tf_op | source)
XLA Modules:
  0.0 277.9 jit_solution(11679175340468570167)
XLA Ops:
  6.5 0.7 all-gather.7.cloned.1.call-update
  7.3 0.0 all-gather.5.cloned.1.call-start
  7.3 0.7 all-gather.5.cloned.1.call-update
  8.0 0.0 copy-done.8
  8.0 0.6 reduce-window.6
  8.6 0.2 slice_reduce_fusion
  8.9 0.1 bitcast_subtract_fusion
  9.0 0.1 copy.61
  9.1 0.1 reshape.236
  9.3 0.2 fusion.24
  9.5 0.2 select_reduce_fusion
  9.7 0.1 reduce_sum.67
  9.8 0.1 broadcast_in_dim.94
  9.9 2.5 gather_fusion
  12.3 1.7 select_select_fusion
  14.1 6.4 %all-to-all-start = ((bf16[8,64,2048]{2,1,0:T(8,128)(2,1)}), bf16[8,64,2048]{2,1,0:T(8,128)(2,1)S(1)}, u32[]{:S(2)}, u32[]{:S(2)}) async-start(bf16[8,64,2048]{2,1,0:T(8,128)(2,1)} %select_select_fusion), calls=%async_computation | async-start | bytes 4194304 | tf_op jit(solution)/shard_map/all_to_all | solution.py:61
  20.4 0.0 all-gather.9.cloned.1.call-start
  20.5 1.5 collective-permute-start
  22.0 40.1 %collective-permute-done = bf16[1,512,1024]{2,1,0:T(8,128)(2,1)S(1)} collective-permute-done((bf16[1,512,1024]{2,1,0:T(8,128)(2,1)}, bf16[1,512,1024]{2,1,0:T(8,128)(2,1)S(1)}, u32[]{:S(2)}, u32[]{:S(2)}) %collective-permute-start) | collective-permute-done | bytes 1048608 | tf_op jit(solution)/shard_map/ppermute | solution.py:78
  62.1 1.0 copy-done.6
  63.1 0.0 collective-permute-start.1
  63.1 38.9 %collective-permute-done.1 = bf16[1,512,1024]{2,1,0:T(8,128)(2,1)} collective-permute-done((bf16[1,512,1024]{2,1,0:T(8,128)(2,1)S(1)}, bf16[1,512,1024]{2,1,0:T(8,128)(2,1)}, u32[]{:S(2)}, u32[]{:S(2)}) %collective-permute-start.1) | collective-permute-done | bytes 1048608 | tf_op jit(solution)/shard_map/ppermute | solution.py:78
  102.0 0.0 collective-permute-start.2
  102.0 0.0 all-to-all-done
  102.1 2.8 fusion.22
  104.8 2.0 fusion.18
  106.9 0.7 fusion.20
  107.6 35.4 %collective-permute-done.2 = bf16[1,512,1024]{2,1,0:T(8,128)(2,1)} collective-permute-done((bf16[1,512,1024]{2,1,0:T(8,128)(2,1)}, bf16[1,512,1024]{2,1,0:T(8,128)(2,1)}, u32[]{:S(2)}, u32[]{:S(2)}) %collective-permute-start.2) | collective-permute-done | bytes 1048608 | tf_op jit(solution)/shard_map/ppermute | solution.py:78
  143.0 2.2 fusion.13
  145.2 0.0 all-gather.7.cloned.1.call-done
  145.2 6.1 %fusion.10 = bf16[512,1024]{1,0:T(8,128)(2,1)} fusion(bf16[512,2048]{1,0:T(8,128)(2,1)} %bitcast.98, bf16[1,2048,1024]{2,1,0:T(8,128)(2,1)} %all-gather.7.cloned.1.call-done), kind=kOutput, calls=%fused_computation.18 | convolution fusion | flops 2148007936 | bytes 7340032 | tf_op jit(solution)/shard_map/mrc,mch->mrh/dot_general | solution.py:66
  151.3 1.5 copy.74
  152.9 1.4 fusion.48
  154.2 0.0 all-gather.9.cloned.1.call-update
  154.3 7.6 %all-gather.5.cloned.1.call-done = bf16[2048,1024]{1,0:T(8,128)(2,1)} async-done(((bf16[512,1024]{1,0:T(8,128)(2,1)}), bf16[2048,1024]{1,0:T(8,128)(2,1)}) %all-gather.5.cloned.1.call-update) | async-done | bytes 4194320 | tf_op jit(solution)/shard_map/all_gather | solution.py:53
  161.9 3.4 %convolution_convert_fusion = bf16[256,1024]{1,0:T(8,128)(2,1)S(1)} fusion(bf16[256,2048]{1,0:T(8,128)(2,1)S(1)} %copy-done, bf16[2048,1024]{1,0:T(8,128)(2,1)} %all-gather.5.cloned.1.call-done), kind=kOutput, calls=%fused_computation.20 | convolution fusion | flops 1074003968 | bytes 5767168 | tf_op jit(solution)/shard_map/dot_general | solution.py:51
  165.3 2.8 %gather_fusion.1 = bf16[512,1024]{1,0:T(8,128)(2,1)} fusion(bf16[256,1024]{1,0:T(8,128)(2,1)S(1)} %convolution_convert_fusion, s32[1024]{0:T(1024)S(1)} %pad_clamp_fusion.1), kind=kCustom, calls=%fused_computation.1 | custom fusion | bytes 2099200 | tf_op jit(solution)/shard_map/jit(_take)/gather | solution.py:57
  168.1 2.5 select_select_fusion.1
  170.6 4.5 %all-to-all-start.1 = ((bf16[8,64,1024]{2,1,0:T(8,128)(2,1)}), bf16[8,64,1024]{2,1,0:T(8,128)(2,1)}, u32[]{:S(2)}, u32[]{:S(2)}) async-start(bf16[8,64,1024]{2,1,0:T(8,128)(2,1)} %select_select_fusion.1), calls=%async_computation.1 | async-start | bytes 2097152 | tf_op jit(solution)/shard_map/all_to_all | solution.py:62
  175.1 1.1 fusion.25
  176.2 13.1 %all-gather.9.cloned.1.call-done = bf16[32,128,128]{2,1,0:T(8,128)(2,1)} async-done(((bf16[8,128,128]{2,1,0:T(8,128)(2,1)}), bf16[32,128,128]{2,1,0:T(8,128)(2,1)}) %all-gather.9.cloned.1.call-update) | async-done | bytes 1048592 | tf_op jit(solution)/shard_map/all_gather | solution.py:15
  189.4 0.2 while.2
  189.6 12.2 %all-to-all-done.1 = bf16[8,64,1024]{2,1,0:T(8,128)(2,1)} async-done(((bf16[8,64,1024]{2,1,0:T(8,128)(2,1)}), bf16[8,64,1024]{2,1,0:T(8,128)(2,1)}, u32[]{:S(2)}, u32[]{:S(2)}) %all-to-all-start.1) | async-done | bytes 1048608 | tf_op jit(solution)/shard_map/all_to_all | solution.py:62
  201.8 1.6 copy.76
  203.3 0.0 copy-start.5
  203.4 1.2 fusion.30
  204.6 1.1 fusion.28
  205.7 0.1 copy-done.4
  205.8 5.5 %fusion.5 = (f32[512,8]{0,1:T(8,128)S(1)}, f32[8,128,512]{2,1,0:T(8,128)S(1)}) fusion(f32[8,128,512]{2,1,0:T(8,128)S(1)} %fusion.28, f32[8,512,512]{2,1,0:T(8,128)S(1)} %fusion.30, f32[512,512]{1,0:T(8,128)S(1)} %copy-done.4, bf16[64,8,8,128]{3,2,1,0:T(8,128)(2,1)S(1)} %fusion.13), kind=kOutput, calls=%fused_computation.11 | convolution fusion | flops 3224891392 | bytes 14696448 | tf_op jit(solution)/shard_map/while/body/eval_jaxpr/hqk,khd->qhd/dot_general | solution.py:116
  211.4 1.3 fusion.6
  212.7 4.7 %copy.70 = bf16[1,512,1024]{2,0,1:T(2,128)(2,1)S(1)} copy(bf16[1,512,1024]{1,2,0:T(8,128)(2,1)} %bitcast.100) | data formatting | bytes 2097152 | tf_op jit(solution)/shard_map/reshape | solution.py:125
  217.4 0.5 broadcast.164
  217.9 7.8 %reduce.2 = bf16[512,1024]{1,0:T(8,128)(2,1)} reduce(bf16[512,1,1024]{2,1,0:T(2,128)(2,1)S(1)} %bitcast.99, bf16[]{:T(256)} %broadcast.164), dimensions={1}, to_apply=%bitcast.73.reduce_sub_computation | reduce | bytes 2097154
  225.7 2.6 reshape.277
  228.4 3.6 %all-to-all-start.2 = ((bf16[8,2,32768]{2,1,0:T(2,128)(2,1)}), bf16[8,2,32768]{2,1,0:T(2,128)(2,1)S(1)}, u32[]{:S(2)}, u32[]{:S(2)}) async-start(bf16[8,2,32768]{2,1,0:T(2,128)(2,1)} %reshape.277), calls=%async_computation.2 | async-start | bytes 2097152 | tf_op jit(solution)/shard_map/all_to_all | solution.py:126
  231.9 0.1 reshape.249
  232.1 0.2 copy.60
  232.3 0.1 copy.59
  232.5 26.0 %all-to-all-done.2 = bf16[8,2,32768]{2,1,0:T(2,128)(2,1)S(1)} async-done(((bf16[8,2,32768]{2,1,0:T(2,128)(2,1)}), bf16[8,2,32768]{2,1,0:T(2,128)(2,1)S(1)}, u32[]{:S(2)}, u32[]{:S(2)}) %all-to-all-start.2) | async-done | bytes 1048608 | tf_op jit(solution)/shard_map/all_to_all | solution.py:126
  258.4 3.5 %reshape.278 = bf16[512,1,1024]{2,1,0:T(2,128)(2,1)} reshape(bf16[8,2,32768]{2,1,0:T(2,128)(2,1)S(1)} %all-to-all-done.2) | data formatting | bytes 2097152
  261.9 2.0 copy.94
  263.8 2.1 gather_fusion.2
  265.9 0.4 gather.23
  266.4 5.0 %multiply_reduce_fusion = bf16[256,1024]{1,0:T(8,128)(2,1)} fusion(bf16[256,2,1024]{2,1,0:T(2,128)(2,1)S(1)} %gather.23, pred[256,2]{1,0:T(8,128)(4,1)S(1)} %copy.60, f32[256,2]{1,0:T(8,128)S(1)} %copy.59), kind=kLoop, calls=%fused_computation.13 | loop fusion | flops 1835008 | bytes 1575424 | tf_op jit(solution)/shard_map/reduce_sum | solution.py:131
  (32 shorter events, 0.2 us)
Async XLA Ops:
  6.5 3.3 %copy-start = (bf16[256,2048]{1,0:T(8,128)(2,1)S(1)}, bf16[256,2048]{1,0:T(8,128)(2,1)}, u32[]{:S(2)}) copy-start(bf16[256,2048]{1,0:T(8,128)(2,1)} %param.8) | copy-start | bytes 3145732
  6.5 1.5 copy-start.8
  6.5 138.7 %all-gather.7.cloned.1.call-start = ((), (), s32[]{:S(2)}) async-start(), calls=%async_computation.4 | async-start | bytes 5242880 | tf_op jit(solution)/shard_map/all_gather | solution.py:69
  7.3 154.6 %all-gather.5.cloned.1.call-start = ((), (), s32[]{:S(2)}) async-start(), calls=%async_computation.3 | async-start | bytes 5242880 | tf_op jit(solution)/shard_map/all_gather | solution.py:53
  14.1 88.0 %all-to-all-start = ((bf16[8,64,2048]{2,1,0:T(8,128)(2,1)}), bf16[8,64,2048]{2,1,0:T(8,128)(2,1)S(1)}, u32[]{:S(2)}, u32[]{:S(2)}) async-start(bf16[8,64,2048]{2,1,0:T(8,128)(2,1)} %select_select_fusion), calls=%async_computation | async-start | bytes 4194304 | tf_op jit(solution)/shard_map/all_to_all | solution.py:61
  20.4 168.9 %all-gather.9.cloned.1.call-start = ((), (), s32[]{:S(2)}) async-start(), calls=%async_computation.5 | async-start | bytes 1310720 | tf_op jit(solution)/shard_map/all_gather | solution.py:15
  20.5 41.7 %collective-permute-start = (bf16[1,512,1024]{2,1,0:T(8,128)(2,1)}, bf16[1,512,1024]{2,1,0:T(8,128)(2,1)S(1)}, u32[]{:S(2)}, u32[]{:S(2)}) collective-permute-start(bf16[1,512,1024]{2,1,0:T(8,128)(2,1)} %param.13), channel_id=1, source_target_pairs={{0,8},{8,16},{16,24},{24,0},{1,9},{9,17},{17,25},{25,1},{2,10},{10... | collective-permute-start | bytes 3145736 | tf_op jit(solution)/shard_map/ppermute | solution.py:78
  62.1 1.0 copy-start.6
  63.1 38.9 %collective-permute-start.1 = (bf16[1,512,1024]{2,1,0:T(8,128)(2,1)S(1)}, bf16[1,512,1024]{2,1,0:T(8,128)(2,1)}, u32[]{:S(2)}, u32[]{:S(2)}) collective-permute-start(bf16[1,512,1024]{2,1,0:T(8,128)(2,1)S(1)} %collective-permute-done), channel_id=1, source_target_pairs={{0,8},{8,16},{16,24},{24,0},{1,9},{9,17},{17,25},{25,1},{2,10},{10... | collective-permute-start | bytes 3145736 | tf_op jit(solution)/shard_map/ppermute | solution.py:78
  102.0 40.9 %collective-permute-start.2 = (bf16[1,512,1024]{2,1,0:T(8,128)(2,1)}, bf16[1,512,1024]{2,1,0:T(8,128)(2,1)}, u32[]{:S(2)}, u32[]{:S(2)}) collective-permute-start(bf16[1,512,1024]{2,1,0:T(8,128)(2,1)} %collective-permute-done.1), channel_id=1, source_target_pairs={{0,8},{8,16},{16,24},{24,0},{1,9},{9,17},{17,25},{25,1},{2,10},{10... | collective-permute-start | bytes 3145736 | tf_op jit(solution)/shard_map/ppermute | solution.py:78
  102.1 4.8 %copy-start.3 = (bf16[8,64,2048]{2,1,0:T(8,128)(2,1)}, bf16[8,64,2048]{2,1,0:T(8,128)(2,1)S(1)}, u32[]{:S(2)}) copy-start(bf16[8,64,2048]{2,1,0:T(8,128)(2,1)S(1)} %all-to-all-done) | copy-start | bytes 6291460
  104.8 2.1 copy-start.7
  152.8 1.4 copy-start.1
  170.6 31.2 %all-to-all-start.1 = ((bf16[8,64,1024]{2,1,0:T(8,128)(2,1)}), bf16[8,64,1024]{2,1,0:T(8,128)(2,1)}, u32[]{:S(2)}, u32[]{:S(2)}) async-start(bf16[8,64,1024]{2,1,0:T(8,128)(2,1)} %select_select_fusion.1), calls=%async_computation.1 | async-start | bytes 2097152 | tf_op jit(solution)/shard_map/all_to_all | solution.py:62
  201.8 1.6 copy-start.2
  203.3 1.3 copy-start.5
  204.6 1.2 copy-start.4
  225.7 6.5 %copy-start.9 = (s32[256,2]{0,1:T(2,128)S(1)}, s32[256,2]{0,1:T(2,128)}, u32[]{:S(2)}) copy-start(s32[256,2]{0,1:T(2,128)} %param.10) | copy-start | bytes 6148
  228.4 30.1 %all-to-all-start.2 = ((bf16[8,2,32768]{2,1,0:T(2,128)(2,1)}), bf16[8,2,32768]{2,1,0:T(2,128)(2,1)S(1)}, u32[]{:S(2)}, u32[]{:S(2)}) async-start(bf16[8,2,32768]{2,1,0:T(2,128)(2,1)} %reshape.277), calls=%async_computation.2 | async-start | bytes 2097152 | tf_op jit(solution)/shard_map/all_to_all | solution.py:126
Sparse Core Ops, SparseCore 0:
  9.2 83.3 all-gather.6
  94.4 67.4 all-gather.4
  163.7 25.5 all-gather.8
